TPU v7x, 256 devices: a whole 4x4x8 slice. The times are simulated.
256 devices in a mesh: ctx: 32 (over z, x), ch: 8 (over y, core).
Axes of the slice: x: 4, y: 4, z: 8, core: 2. Of those that a mesh axis runs over, the one named last changes fastest.
Arguments:
- featurized: bfloat16 [3, 1024, 16384], P(None, 'ch', 'ctx'), may hold values from -6 to 6
- short_weights: float32 [3, 1024, 3], P(None, 'ch'), may hold values from -3.5 to 3.5
- filter_taps: float32 [1024, 16384], P('ch', 'ctx'), may hold values from -5 to 5
- skip_gain: float32 [1024], P('ch'), may hold values from 0.5 to 1.5
- w_out: bfloat16 [1024, 1024], P('ch'), may hold values from -0.1875 to 0.1875
Outputs:
- mixed: bfloat16 [1024, 16384], P('ch', 'ctx')
All inputs are finite; a program needn't handle non-finite values.
Results may differ from a plain program's by a relative error of at most 0.0089.
Values may be sent and summed in bfloat16 or wider, within the bound.
A program may use at most 64 MiB of HBM per device.

v0:
```python
import math

import jax
import jax.numpy as jnp
import numpy as np
from jax import lax
from jax.experimental import pallas as pl
from jax.experimental.pallas import tpu as pltpu
from jax.sharding import PartitionSpec as P

NP = 32
NC = 4
MESH = pl.DeviceIdType.MESH
F32 = jnp.float32
BF16 = jnp.bfloat16


def split(table):
    high = table.astype(BF16)
    return high, (table - high.astype(np.float32)).astype(BF16)


def tables():
    index = np.arange(128)
    first = 4 * (index % NP) + index // NP
    one = 2 * math.pi * (((4 * index[:, None] + 1) * first[None, :]) % 512) / 512
    two = 2 * math.pi * ((index[:, None] * index[None, :]) % 128) / 128
    twist = 2 * math.pi * (((4 * index[:, None] + 1) * index[None, :]) % 65536) / 65536
    c2, s2 = np.cos(two), np.sin(two)
    f32 = np.float32
    e1 = np.concatenate([np.cos(one), -np.sin(one)], 0).astype(f32)
    m2 = np.block([[c2, -s2], [s2, c2]]).astype(f32)
    m3 = np.block([[c2, s2], [-s2, c2]]).astype(f32)
    back = (np.concatenate([np.cos(one).T, -np.sin(one).T], 1) / 16384).astype(f32)
    e1_high, e1_low = split(e1)
    return (
        np.concatenate([e1_high, e1_low], 1),
        np.stack(split(m2)),
        np.stack(split(m3)),
        np.stack(split(back)),
        np.stack([np.cos(twist), -np.sin(twist)]).astype(f32),
    )


def dot(left, right):
    return jnp.dot(left, right, preferred_element_type=F32)


def halves(value):
    high = value.astype(BF16)
    return high, (value - high.astype(F32)).astype(BF16)


def forward(rows, e1, m2, twist):
    parts = []
    for c in range(NC):
        parts.append(
            jnp.concatenate([rows[pl.ds(4 * c + a, NP, stride=16), :] for a in range(4)], 0)
        )
    grid = jnp.concatenate(parts, 1).astype(BF16)
    mixed = dot(e1[...], jnp.concatenate([grid, grid], 0))
    tr, ti = twist[0], twist[1]
    turned = []
    for c in range(NC):
        re, im = mixed[:128, 128 * c : 128 * c + 128], mixed[128:, 128 * c : 128 * c + 128]
        turned.append(jnp.concatenate([re * tr - im * ti, re * ti + im * tr], 1))
    high, low = halves(jnp.concatenate(turned, 0))
    return dot(high, m2[0]) + dot(low, m2[0]) + dot(high, m2[1])


def inverse(spectrum, rows, m3, back, twist):
    high, low = halves(spectrum)
    mixed = dot(high, m3[0]) + dot(low, m3[0]) + dot(high, m3[1])
    tr, ti = twist[0], twist[1]
    turned = []
    for c in range(NC):
        re, im = mixed[128 * c : 128 * c + 128, :128], mixed[128 * c : 128 * c + 128, 128:]
        turned.append(jnp.concatenate([re * tr + im * ti, im * tr - re * ti], 0))
    high, low = halves(jnp.concatenate(turned, 1))
    done = dot(back[0], high) + dot(back[1], high) + dot(back[0], low)
    for c in range(NC):
        for a in range(4):
            rows[pl.ds(4 * c + a, NP, stride=16), :] = done[
                NP * a : NP * a + NP, 128 * c : 128 * c + 128
            ]


def product(g, h):
    gr, gi, hr, hi = g[:, :128], g[:, 128:], h[:, :128], h[:, 128:]
    return jnp.concatenate([gr * hr - gi * hi, gr * hi + gi * hr], 1)


def kernel(
    feat, taps, sw, skip, w, e1h, m2h, m3h, bkh, twh, out,
    fv, tv, swv, skv, wv, e1, m2, m3, bk, tw,
    halo, cols, f0, gt, rows, hsend, hrecv, gsend, grecv, csend, crecv, spec, ag,
    lsem, osem, rsem, asem, arem,
):
    me = lax.axis_index("ctx")
    ch = lax.axis_index("ch")
    y, core = ch // 2, ch % 2
    partner = 2 * y + 1 - core
    up, down = (y + 1) % 4 * 2 + core, (y + 3) % 4 * 2 + core
    across = (y + 2) % 4 * 2 + core

    local = [
        pltpu.make_async_copy(s, d, lsem.at[i])
        for i, (s, d) in enumerate(
            [(taps, tv), (feat, fv), (sw, swv), (skip, skv), (e1h, e1), (m2h, m2), (twh, tw),
             (m3h, m3), (bkh, bk), (w, wv)]
        )
    ]
    for c in local:
        c.start()

    barrier = pltpu.get_barrier_semaphore()

    def greet(i, _):
        pl.semaphore_signal(
            barrier, inc=1, device_id={"ctx": (me + i) % NP}, device_id_type=MESH
        )
        return 0

    lax.fori_loop(1, NP, greet, 0)
    for other in (partner, up, down):
        pl.semaphore_signal(barrier, inc=1, device_id={"ch": other}, device_id_type=MESH)

    def lay(ref, send):
        send[...] = ref[...].astype(BF16).reshape(NP, 16, 128)

    local[0].wait()
    for a in range(4):
        rows[pl.ds(a, 128, stride=4), :] = tv[:, 128 * a : 128 * a + 128]
    lay(rows, hsend)
    hrecv[me] = hsend[me]
    local[1].wait()
    pl.semaphore_wait(barrier, NP - 1 + 3)

    rim = pltpu.make_async_remote_copy(
        fv.at[:, :, pl.ds(384, 128)], halo, osem.at[3], rsem.at[3],
        device_id={"ctx": (me + 1) % NP}, device_id_type=MESH,
    )
    rim.start()

    def spread(send, recv, k):
        def one(i, _):
            peer = (me + i) % NP
            pltpu.make_async_remote_copy(
                send.at[peer], recv.at[me], osem.at[k], rsem.at[k],
                device_id={"ctx": peer}, device_id_type=MESH,
            ).start()
            return 0

        lax.fori_loop(1, NP, one, 0)

    def arrived(buf, sem):
        part = buf.at[pl.ds(0, NP - 1)]
        pltpu.make_async_copy(part, part, sem).wait()

    spread(hsend, hrecv, 0)

    local[2].wait()
    local[3].wait()
    cols[...] = jnp.zeros_like(cols)
    for s in range(3):
        for j in range(3):
            cols[pl.ds(3 * s + j, 1), :] = swv[s, pl.ds(j, 1), :]
    cols[pl.ds(9, 1), :] = skv[...]
    col = cols[...].T
    rim.wait()
    inside = me > 0

    def short(s):
        edge = jnp.where(inside, halo[s].astype(F32), 0.0)
        wide = jnp.concatenate([edge, fv[s].astype(F32)], 1)
        total = col[:, 3 * s : 3 * s + 1] * wide[:, 128:]
        for j in (1, 2):
            moved = pltpu.roll(wide, j, 1)[:, 128:]
            total = total + col[:, 3 * s + j : 3 * s + j + 1] * moved
        return total

    gt[...] = short(1) * short(2)
    for a in range(4):
        rows[pl.ds(a, 128, stride=4), :] = gt[:, 128 * a : 128 * a + 128]
    lay(rows, gsend)
    grecv[me] = gsend[me]
    spread(gsend, grecv, 1)
    f0[...] = short(0)
    gt[...] = col[:, 9:10] * gt[...]

    for c in local[4:]:
        c.wait()
    arrived(hrecv, rsem.at[0])
    rows[...] = hrecv[...].reshape(512, 128).astype(F32)
    spec[...] = forward(rows, e1, m2, tw)
    arrived(grecv, rsem.at[1])
    rows[...] = grecv[...].reshape(512, 128).astype(F32)
    inverse(product(forward(rows, e1, m2, tw), spec[...]), rows, m3, bk, tw)
    lay(rows, csend)
    crecv[me] = csend[me]
    spread(csend, crecv, 2)
    arrived(crecv, rsem.at[2])

    rows[...] = crecv[...].reshape(512, 128).astype(F32)
    for a in range(4):
        lanes = pl.ds(128 * a, 128)
        conv = rows[pl.ds(a, 128, stride=4), :]
        ag[ch, :, lanes] = (f0[:, lanes] * (conv + gt[:, lanes])).astype(BF16)

    def hand(block, half, k, other):
        piece = ag.at[block, pl.ds(64 * half, 64)]
        return pltpu.make_async_remote_copy(
            piece, piece, asem.at[k], arem.at[k], device_id={"ch": other}, device_id_type=MESH
        )

    sent = []

    def go(*args):
        copy = hand(*args)
        copy.start()
        sent.append(copy)

    def take(block, half, k):
        hand(block, half, k, partner).wait_recv()

    go(ch, 0, 0, up)
    go(ch, 1, 1, down)
    go(ch, 1, 2, up)
    go(ch, 0, 3, down)
    go(ch, 0, 4, partner)
    go(ch, 1, 5, partner)
    take(down, 0, 0)
    go(down, 0, 6, up)
    take(up, 1, 1)
    go(up, 1, 7, down)
    go(down, 0, 8, partner)
    go(up, 1, 9, partner)
    take(down, 1, 2)
    go(down, 1, 10, partner)
    take(up, 0, 3)
    go(up, 0, 11, partner)
    take(partner, 0, 4)
    take(partner, 1, 5)

    def pair(chip):
        both = ag[pl.ds(2 * chip, 2)].reshape(256, 512)
        return dot(wv[:, pl.ds(pl.multiple_of(256 * chip, 256), 256)], both)

    total = pair(y)
    twin_up, twin_down, twin_across = ((x // 2) * 2 + 1 - core for x in (up, down, across))
    take(across, 0, 6)
    go(across, 0, 12, partner)
    take(across, 1, 7)
    go(across, 1, 13, partner)
    take(twin_down, 0, 8)
    take(twin_up, 1, 9)
    take(twin_down, 1, 10)
    take(twin_up, 0, 11)
    total = total + pair(up // 2) + pair(down // 2)
    take(twin_across, 0, 12)
    take(twin_across, 1, 13)
    out[...] = (total + pair(across // 2)).astype(BF16)

    for copy in sent:
        copy.wait_send()
    arrived(hsend, osem.at[0])
    arrived(gsend, osem.at[1])
    arrived(csend, osem.at[2])


def local(featurized, short_weights, filter_taps, skip_gain, w_out):
    e1, m2, m3, back, twist = tables()
    any_space = pl.BlockSpec(memory_space=pl.ANY)
    V = pltpu.VMEM
    chunk = V((NP, 16, 128), BF16)
    return pl.pallas_call(
        kernel,
        out_shape=jax.ShapeDtypeStruct((128, 512), BF16),
        in_specs=[any_space] * 10,
        out_specs=pl.BlockSpec(memory_space=pltpu.VMEM),
        scratch_shapes=[
            V((3, 128, 512), BF16), V((128, 512), F32), V((3, 3, 128), F32), V((1, 128), F32),
            V((128, 1024), BF16), V(e1.shape, BF16), V(m2.shape, BF16), V(m3.shape, BF16),
            V(back.shape, BF16), V(twist.shape, F32),
            V((3, 128, 128), BF16), V((128, 128), F32), V((128, 512), F32), V((128, 512), F32),
            V((512, 128), F32), chunk, chunk, chunk, chunk, chunk, chunk,
            V((512, 256), F32), V((8, 128, 512), BF16),
            pltpu.SemaphoreType.DMA((10,)),
            pltpu.SemaphoreType.DMA((4,)),
            pltpu.SemaphoreType.DMA((4,)),
            pltpu.SemaphoreType.DMA((14,)),
            pltpu.SemaphoreType.DMA((14,)),
        ],
        compiler_params=pltpu.CompilerParams(collective_id=0, has_side_effects=True),
        name="hyena",
    )(
        featurized, filter_taps, jnp.swapaxes(short_weights, 1, 2), skip_gain.reshape(1, 128),
        w_out, e1, m2, m3, back, twist,
    )


def solution(mesh):
    in_specs = (P(None, "ch", "ctx"), P(None, "ch", None), P("ch", "ctx"), P("ch"), P("ch", None))
    out_specs = P("ch", "ctx")
    return jax.shard_map(local, mesh=mesh, in_specs=in_specs, out_specs=out_specs, check_vma=False)
```

profile of v0, /device:TPU:1, one launch (start us, length us, event | category | flops | bytes accessed | tf_op | source)
XLA Modules:
  0.0 44.3 jit_solution(17080168588350877043)
XLA Ops:
  0.0 42.7 %hyena.1 = bf16[128,512]{1,0:T(8,128)(2,1)} custom-call(bf16[3,128,512]{2,1,0:T(8,128)(2,1)} %feat.1, f32[128,512]{1,0:T(8,128)} %taps.1, f32[3,3,128]{2,1,0:T(4,128)} %bitcast.2, f32[1,128]{1,0:T(1,128)} %bitcast.3, bf16[128,1024]{1,0:T(8,128)(2,1)} %w.1, bf16[256,256]{1,0:T(8,128)(2,1)} %constant.10.clone.e1h, bf16[2,256,256]{2,1,0:T(8,128)(2,1)} %constant.11.clone.m2h, ...), custom_call_target="tpu_custom_call" | custom-call | tf_op jit(solution)/shard_map/hyena/pallas_call | solution.py:276
  42.7 1.6 %copy.12 = bf16[128,512]{1,0:T(8,128)(2,1)} copy(bf16[128,512]{1,0:T(8,128)(2,1)} %hyena.1) | data formatting | bytes 262144
where the time goes:
time: 44.4 us; the launch traced here: 44.3 us
  Pallas kernels  42.7 us (96%)
  local copies, waits for them, and re-layouts  1.57 us (4%)
    pallas_call x1, Pallas kernels, local(): pl.pallas_call(kernel, out_shape=jax.ShapeDtypeStruct((128, 512), BF16),...  42.7 us
    unnamed x1, local copies, waits for them, and re-layouts  1.57 us

commit v1 on v0

v1 whole, which is shorter than its diff:
```python
import math

import jax
import jax.numpy as jnp
import numpy as np
from jax import lax
from jax.experimental import pallas as pl
from jax.experimental.pallas import tpu as pltpu
from jax.sharding import PartitionSpec as P

NP = 32
NC = 4
FAR_H, FAR_G, FAR_C = False, True, False
MESH = pl.DeviceIdType.MESH
F32 = jnp.float32
BF16 = jnp.bfloat16


def split(table):
    high = table.astype(BF16)
    return high, (table - high.astype(np.float32)).astype(BF16)


def tables():
    index = np.arange(128)
    first = 4 * (index % NP) + index // NP
    one = 2 * math.pi * (((4 * index[:, None] + 1) * first[None, :]) % 512) / 512
    two = 2 * math.pi * ((index[:, None] * index[None, :]) % 128) / 128
    twist = 2 * math.pi * (((4 * index[:, None] + 1) * index[None, :]) % 65536) / 65536
    c2, s2 = np.cos(two), np.sin(two)
    f32 = np.float32
    e1 = np.concatenate([np.cos(one), -np.sin(one)], 0).astype(f32)
    m2 = np.block([[c2, -s2], [s2, c2]]).astype(f32)
    m3 = np.block([[c2, s2], [-s2, c2]]).astype(f32)
    back = (np.concatenate([np.cos(one).T, -np.sin(one).T], 1) / 16384).astype(f32)
    e1_high, e1_low = split(e1)
    return (
        np.concatenate([e1_high, e1_low], 1),
        np.stack(split(m2)),
        np.stack(split(m3)),
        np.stack(split(back)),
        np.stack([np.cos(twist), -np.sin(twist)]).astype(f32),
    )


def dot(left, right):
    return jnp.dot(left, right, preferred_element_type=F32)


def halves(value):
    high = value.astype(BF16)
    return high, (value - high.astype(F32)).astype(BF16)


def forward(rows, e1, m2, twist):
    parts = []
    for c in range(NC):
        parts.append(
            jnp.concatenate([rows[pl.ds(4 * c + a, NP, stride=16), :] for a in range(4)], 0)
        )
    grid = jnp.concatenate(parts, 1).astype(BF16)
    mixed = dot(e1[...], jnp.concatenate([grid, grid], 0))
    tr, ti = twist[0], twist[1]
    turned = []
    for c in range(NC):
        re, im = mixed[:128, 128 * c : 128 * c + 128], mixed[128:, 128 * c : 128 * c + 128]
        turned.append(jnp.concatenate([re * tr - im * ti, re * ti + im * tr], 1))
    high, low = halves(jnp.concatenate(turned, 0))
    return dot(high, m2[0]) + dot(low, m2[0]) + dot(high, m2[1])


def inverse(spectrum, rows, m3, back, twist):
    high, low = halves(spectrum)
    mixed = dot(high, m3[0]) + dot(low, m3[0]) + dot(high, m3[1])
    tr, ti = twist[0], twist[1]
    turned = []
    for c in range(NC):
        re, im = mixed[128 * c : 128 * c + 128, :128], mixed[128 * c : 128 * c + 128, 128:]
        turned.append(jnp.concatenate([re * tr + im * ti, im * tr - re * ti], 0))
    high, low = halves(jnp.concatenate(turned, 1))
    done = dot(back[0], high) + dot(back[1], high) + dot(back[0], low)
    for c in range(NC):
        for a in range(4):
            rows[pl.ds(a // 2 * 8 + 2 * c + a % 2, NP, stride=16), :] = done[
                NP * a : NP * a + NP, 128 * c : 128 * c + 128
            ]


def product(g, h):
    gr, gi, hr, hi = g[:, :128], g[:, 128:], h[:, :128], h[:, 128:]
    return jnp.concatenate([gr * hr - gi * hi, gr * hi + gi * hr], 1)


def plane_order(k):
    return (k + 1) // 2 * (2 * (k % 2) - 1)


def kernel(
    feat, taps, sw, skip, w, e1h, m2h, m3h, bkh, twh, out,
    fv, tv, swv, skv, wv, wr, e1, m2, m3, bk, tw,
    rimsend, rimrecv, cols, f0, gt, f0r, gtr, rows,
    hsend, hrecv, gsend, grecv, csend, crecv, spec, ag, fin, finr,
    lsem, osem, rsem, csem, asem, arem, psem, prem,
):
    me = lax.axis_index("ctx")
    ch = lax.axis_index("ch")
    x, z = me % 4, me // 4
    y, core = ch // 2, ch % 2
    partner = 2 * y + 1 - core
    up, down, across = ((y + d) % 4 * 2 + core for d in (1, 3, 2))

    local = [
        pltpu.make_async_copy(s, d, lsem.at[i])
        for i, (s, d) in enumerate(
            [(taps, tv), (feat, fv), (sw, swv), (skip, skv), (w, wv), (e1h, e1), (m2h, m2), (twh, tw),
             (m3h, m3), (bkh, bk)]
        )
    ]
    for c in local:
        c.start()

    barrier = pltpu.get_barrier_semaphore()

    def greet(i, _):
        for own in (ch, partner):
            pl.semaphore_signal(
                barrier, inc=1, device_id={"ctx": (me + i) % NP, "ch": own}, device_id_type=MESH
            )
        return 0

    lax.fori_loop(1, NP, greet, 0)
    for other in (partner, up, down, across):
        pl.semaphore_signal(barrier, inc=1, device_id={"ch": other}, device_id_type=MESH)

    local[0].wait()
    for a in range(4):
        rows[pl.ds(a, 128, stride=4), :] = tv[:, 128 * a : 128 * a + 128]
    hsend[...] = rows[...].astype(BF16).reshape(NP, 16, 128)
    hrecv[me] = hsend[me]
    local[1].wait()
    for s in range(3):
        rimsend[pl.ds(8 * s, 8), :] = fv[s, :, 384:].astype(F32).T[120:, :]
    local[4].wait()

    pl.semaphore_wait(barrier, 2 * (NP - 1) + 4)
    rim = pltpu.make_async_remote_copy(
        rimsend, rimrecv, osem.at[3], rsem.at[3],
        device_id={"ctx": (me + 1) % NP}, device_id_type=MESH,
    )
    rim.start()

    def spot(i, far):
        i = NP - i if far else i
        return (z + 8 + plane_order(i // 4)) % 8 * 4 + (x + i) % 4

    def spread(send, recv, k, far):
        def one(i, _):
            peer = spot(i, far)
            pltpu.make_async_remote_copy(
                send.at[peer], recv.at[me], osem.at[k], rsem.at[k],
                device_id={"ctx": peer}, device_id_type=MESH,
            ).start()
            return 0

        lax.fori_loop(1, NP, one, 0)

    def arrived(part, sem):
        pltpu.make_async_copy(part, part, sem).wait()

    def mates(i, source, target):
        return pltpu.make_async_remote_copy(
            source, target, psem.at[i], prem.at[i], device_id={"ch": partner}, device_id_type=MESH
        )

    most = pl.ds(0, NP - 1)
    spread(hsend, hrecv, 0, FAR_H)
    swap = [mates(0, wv, wr)]
    swap[0].start()

    local[2].wait()
    local[3].wait()
    cols[...] = jnp.zeros_like(cols)
    for s in range(3):
        for j in range(3):
            cols[pl.ds(3 * s + j, 1), :] = swv[s, pl.ds(j, 1), :]
    cols[pl.ds(9, 1), :] = skv[...]
    col = cols[...].T

    def short(s, edge, width):
        wide = jnp.concatenate([edge, fv[s, :, :width].astype(F32)], 1)
        total = col[:, 3 * s : 3 * s + 1] * wide[:, 128:]
        for j in (1, 2):
            moved = pltpu.roll(wide, j, 1)[:, 128:]
            total = total + col[:, 3 * s + j : 3 * s + j + 1] * moved
        return total

    nothing = jnp.zeros((128, 128), F32)
    gated = short(1, nothing, 512) * short(2, nothing, 512)
    gt[0], gt[1] = gated[:, :256], gated[:, 256:]
    for a in range(1, 4):
        rows[pl.ds(a, 128, stride=4), :] = gated[:, 128 * a : 128 * a + 128]

    rim.wait()
    inside = me > 0

    def edge(s):
        last = jnp.concatenate([jnp.zeros((120, 128), F32), rimrecv[pl.ds(8 * s, 8), :]], 0)
        return jnp.where(inside, last.T, 0.0)

    gt[0, :, :128] = short(1, edge(1), 128) * short(2, edge(2), 128)
    rows[pl.ds(0, 128, stride=4), :] = gt[0, :, :128]
    gsend[...] = rows[...].astype(BF16).reshape(NP, 16, 128)
    grecv[me] = gsend[me]
    spread(gsend, grecv, 1, FAR_G)
    for half in range(2):
        gt[half] = col[:, 9:10] * gt[half]
    whole = short(0, edge(0), 512)
    f0[0], f0[1] = whole[:, :256], whole[:, 256:]
    swap += [mates(1, gt.at[1 - core], gtr), mates(2, f0.at[1 - core], f0r)]
    swap[1].start()
    swap[2].start()

    for c in local[5:]:
        c.wait()
    arrived(hrecv.at[most], rsem.at[0])
    rows[...] = hrecv[...].reshape(512, 128).astype(F32)
    spec[...] = forward(rows, e1, m2, tw)
    for c in swap:
        c.wait_recv()
    arrived(grecv.at[most], rsem.at[1])
    rows[...] = grecv[...].reshape(512, 128).astype(F32)
    inverse(product(forward(rows, e1, m2, tw), spec[...]), rows, m3, bk, tw)

    csend[...] = rows[...].astype(BF16).reshape(NP, 2, 8, 128)
    crecv[core, me] = csend[me, core]

    def half_of(peer, half, sem):
        pltpu.make_async_remote_copy(
            csend.at[peer, half], crecv.at[core, me], sem, csem.at[z],
            device_id={"ctx": peer, "ch": 2 * y + half}, device_id_type=MESH,
        ).start()

    half_of(me, 1 - core, osem.at[4])

    def one(i, _):
        for half in range(2):
            half_of(spot(i, FAR_C), half, osem.at[2])
        return 0

    lax.fori_loop(1, NP, one, 0)

    def plane(k):
        return (z + 8 + plane_order(k)) % 8

    def hand(chip, k, t, other):
        piece = ag.at[pl.ds(2 * chip, 2), pl.ds(pl.multiple_of(16 * plane(k), 16), 16)]
        return pltpu.make_async_remote_copy(
            piece, piece, asem.at[t, k], arem.at[t, k], device_id={"ch": other}, device_id_type=MESH
        )

    sent = []
    for k in (range(7, -1, -1) if FAR_C else range(8)):
        first = plane(k)
        arrived(crecv.at[0, pl.ds(0, 8 if k else 7)], csem.at[first])
        here = pl.ds(pl.multiple_of(16 * first, 16), 16)
        for which, (block, f, g) in enumerate(
            [(core, f0.at[core], gt.at[core]), (1 - core, f0r, gtr)]
        ):
            base = 64 * k + 32 * which
            came = crecv[block, pl.ds(4 * first, 4)].reshape(32, 128)
            rows[pl.ds(base, 32), :] = came.astype(F32)
            for a in range(2):
                lanes = pl.ds(128 * a, 128)
                conv = rows[pl.ds(base + a, 16, stride=2), :]
                ag[2 * y + block, here, lanes] = (
                    f[here, lanes] * (conv + g[here, lanes])
                ).astype(BF16)
        for t, other in ((2, across), (0, up), (1, down)):
            copy = hand(y, k, t, other)
            copy.start()
            sent.append(copy)

    def pair(chip):
        both = ag[pl.ds(2 * chip, 2)].reshape(256, 256)
        columns = pl.ds(pl.multiple_of(256 * chip, 256), 256)
        return dot(jnp.concatenate([wr[:, columns], wv[:, columns]], 0), both)

    total = pair(y)
    for t, other in ((0, down), (1, up), (2, across)):
        for k in range(8):
            hand(other // 2, k, t, other).wait_recv()
        total = total + pair(other // 2)
    fin[...] = total[:128].astype(BF16)
    last = mates(3, fin, finr)
    last.start()
    mine = total[128:].astype(BF16)
    out[:, pl.ds(pl.multiple_of(256 * core, 256), 256)] = mine
    last.wait_recv()
    out[:, pl.ds(pl.multiple_of(256 * (1 - core), 256), 256)] = finr[...]

    for copy in sent + swap + [last]:
        copy.wait_send()
    arrived(hsend.at[most], osem.at[0])
    arrived(gsend.at[most], osem.at[1])
    arrived(csend.at[most], osem.at[2])
    arrived(csend.at[0, 0], osem.at[4])


def local(featurized, short_weights, filter_taps, skip_gain, w_out):
    e1, m2, m3, back, twist = tables()
    far = pl.BlockSpec(memory_space=pl.ANY)
    V = pltpu.VMEM
    chunk = V((NP, 16, 128), BF16)
    two = V((2, 128, 256), F32)
    half = V((128, 256), F32)
    return pl.pallas_call(
        kernel,
        out_shape=jax.ShapeDtypeStruct((128, 512), BF16),
        in_specs=[far] * 10,
        out_specs=pl.BlockSpec(memory_space=pltpu.VMEM),
        scratch_shapes=[
            V((3, 128, 512), BF16), V((128, 512), F32), V((3, 3, 128), F32), V((1, 128), F32),
            V((128, 1024), BF16), V((128, 1024), BF16),
            V(e1.shape, BF16), V(m2.shape, BF16), V(m3.shape, BF16),
            V(back.shape, BF16), V(twist.shape, F32),
            V((24, 128), F32), V((24, 128), F32), V((128, 128), F32),
            two, two, half, half, V((512, 128), F32), chunk, chunk, chunk, chunk,
            V((NP, 2, 8, 128), BF16), V((2, NP, 8, 128), BF16),
            V((512, 256), F32), V((8, 128, 256), BF16), V((128, 256), BF16), V((128, 256), BF16),
            pltpu.SemaphoreType.DMA((10,)),
            pltpu.SemaphoreType.DMA((5,)),
            pltpu.SemaphoreType.DMA((4,)),
            pltpu.SemaphoreType.DMA((8,)),
            pltpu.SemaphoreType.DMA((3, 8)),
            pltpu.SemaphoreType.DMA((3, 8)),
            pltpu.SemaphoreType.DMA((4,)),
            pltpu.SemaphoreType.DMA((4,)),
        ],
        compiler_params=pltpu.CompilerParams(collective_id=0, has_side_effects=True),
        name="hyena",
    )(
        featurized, filter_taps, jnp.swapaxes(short_weights, 1, 2), skip_gain.reshape(1, 128),
        w_out, e1, m2, m3, back, twist,
    )


def solution(mesh):
    in_specs = (P(None, "ch", "ctx"), P(None, "ch", None), P("ch", "ctx"), P("ch"), P("ch", None))
    out_specs = P("ch", "ctx")
    return jax.shard_map(local, mesh=mesh, in_specs=in_specs, out_specs=out_specs, check_vma=False)
```

time: 44.4 us -> 40.9 us (0.921)
  Pallas kernels: 42.7 us -> 39.2 us
    pallas_call x1, Pallas kernels: 42.7 us -> 39.2 us  [local(): pl.pallas_call(kernel, out_shape=jax.ShapeDtypeStruct((128, 512), BF16),...]
where the time goes in v1:
time: 40.9 us; the launch traced here: 40.7 us
  Pallas kernels  39.2 us (96%)
  local copies, waits for them, and re-layouts  1.57 us (4%)
    pallas_call x1, Pallas kernels, local(): pl.pallas_call(kernel, out_shape=jax.ShapeDtypeStruct((128, 512), BF16),...  39.2 us
    unnamed x1, local copies, waits for them, and re-layouts  1.57 us

profile of v1, /device:TPU:1, one launch (start us, length us, event | category | flops | bytes accessed | tf_op | source)
XLA Modules:
  0.0 40.7 jit_solution(8816942261456759520)
XLA Ops:
  0.0 39.2 %hyena.1 = bf16[128,512]{1,0:T(8,128)(2,1)} custom-call(bf16[3,128,512]{2,1,0:T(8,128)(2,1)} %feat.1, f32[128,512]{1,0:T(8,128)} %taps.1, f32[3,3,128]{2,1,0:T(4,128)} %bitcast.2, f32[1,128]{1,0:T(1,128)} %bitcast.3, bf16[128,1024]{1,0:T(8,128)(2,1)} %w.1, bf16[256,256]{1,0:T(8,128)(2,1)} %constant.10.clone.e1h, bf16[2,256,256]{2,1,0:T(8,128)(2,1)} %constant.11.clone.m2h, ...), custom_call_target="tpu_custom_call" | custom-call | tf_op jit(solution)/shard_map/hyena/pallas_call | solution.py:316
  39.2 1.6 %copy.12 = bf16[128,512]{1,0:T(8,128)(2,1)} copy(bf16[128,512]{1,0:T(8,128)(2,1)} %hyena.1) | data formatting | bytes 262144

commit v2 on v1

--- a/solution.py
+++ b/solution.py
@@ -92,7 +92,7 @@
 
 
 def plane_order(k):
-    return (k + 1) // 2 * (2 * (k % 2) - 1)
+    return lax.div(k + 1, 2) * (2 * lax.rem(k, 2) - 1)
 
 
 def kernel(
@@ -104,10 +104,31 @@
 ):
     me = lax.axis_index("ctx")
     ch = lax.axis_index("ch")
-    x, z = me % 4, me // 4
-    y, core = ch // 2, ch % 2
+    x, z = lax.rem(me, 4), lax.div(me, 4)
+    y, core = lax.div(ch, 2), lax.rem(ch, 2)
     partner = 2 * y + 1 - core
-    up, down, across = ((y + d) % 4 * 2 + core for d in (1, 3, 2))
+    up, down, across = (2 * lax.rem(y + d, 4) + core for d in (1, 3, 2))
+    row = [lax.rem(x + d, 4) for d in range(4)]
+
+    def plane(k):
+        return lax.rem(z + 8 + plane_order(k), 8)
+
+    def visit(do, far):
+        def one(k, _):
+            base = 4 * plane(8 - k if far else k)
+            for d in (2, 1, 3, 0):
+                do(base + row[d])
+            return 0
+
+        def own():
+            for d in (2, 1, 3):
+                do(4 * z + row[d])
+
+        if not far:
+            own()
+        lax.fori_loop(1, 8, one, 0)
+        if far:
+            own()
 
     local = [
         pltpu.make_async_copy(s, d, lsem.at[i])
@@ -121,14 +142,13 @@
 
     barrier = pltpu.get_barrier_semaphore()
 
-    def greet(i, _):
+    def greet(peer):
         for own in (ch, partner):
             pl.semaphore_signal(
-                barrier, inc=1, device_id={"ctx": (me + i) % NP, "ch": own}, device_id_type=MESH
+                barrier, inc=1, device_id={"ctx": peer, "ch": own}, device_id_type=MESH
             )
-        return 0
-
-    lax.fori_loop(1, NP, greet, 0)
+
+    visit(greet, True)
     for other in (partner, up, down, across):
         pl.semaphore_signal(barrier, inc=1, device_id={"ch": other}, device_id_type=MESH)
 
@@ -140,29 +160,22 @@
     local[1].wait()
     for s in range(3):
         rimsend[pl.ds(8 * s, 8), :] = fv[s, :, 384:].astype(F32).T[120:, :]
-    local[4].wait()
 
     pl.semaphore_wait(barrier, 2 * (NP - 1) + 4)
     rim = pltpu.make_async_remote_copy(
         rimsend, rimrecv, osem.at[3], rsem.at[3],
-        device_id={"ctx": (me + 1) % NP}, device_id_type=MESH,
+        device_id={"ctx": lax.rem(me + 1, NP)}, device_id_type=MESH,
     )
     rim.start()
 
-    def spot(i, far):
-        i = NP - i if far else i
-        return (z + 8 + plane_order(i // 4)) % 8 * 4 + (x + i) % 4
-
     def spread(send, recv, k, far):
-        def one(i, _):
-            peer = spot(i, far)
+        def one(peer):
             pltpu.make_async_remote_copy(
                 send.at[peer], recv.at[me], osem.at[k], rsem.at[k],
                 device_id={"ctx": peer}, device_id_type=MESH,
             ).start()
-            return 0
-
-        lax.fori_loop(1, NP, one, 0)
+
+        visit(one, far)
 
     def arrived(part, sem):
         pltpu.make_async_copy(part, part, sem).wait()
@@ -174,6 +187,7 @@
 
     most = pl.ds(0, NP - 1)
     spread(hsend, hrecv, 0, FAR_H)
+    local[4].wait()
     swap = [mates(0, wv, wr)]
     swap[0].start()
 
@@ -242,25 +256,23 @@
 
     half_of(me, 1 - core, osem.at[4])
 
-    def one(i, _):
+    def both_of(peer):
         for half in range(2):
-            half_of(spot(i, FAR_C), half, osem.at[2])
-        return 0
-
-    lax.fori_loop(1, NP, one, 0)
-
-    def plane(k):
-        return (z + 8 + plane_order(k)) % 8
+            half_of(peer, half, osem.at[2])
+
+    visit(both_of, FAR_C)
+
+    planes = [lax.rem(z + d, 8) for d in (0, 1, 7, 2, 6, 3, 5, 4)]
 
     def hand(chip, k, t, other):
-        piece = ag.at[pl.ds(2 * chip, 2), pl.ds(pl.multiple_of(16 * plane(k), 16), 16)]
+        piece = ag.at[pl.ds(2 * chip, 2), pl.ds(pl.multiple_of(16 * planes[k], 16), 16)]
         return pltpu.make_async_remote_copy(
             piece, piece, asem.at[t, k], arem.at[t, k], device_id={"ch": other}, device_id_type=MESH
         )
 
     sent = []
     for k in (range(7, -1, -1) if FAR_C else range(8)):
-        first = plane(k)
+        first = planes[k]
         arrived(crecv.at[0, pl.ds(0, 8 if k else 7)], csem.at[first])
         here = pl.ds(pl.multiple_of(16 * first, 16), 16)
         for which, (block, f, g) in enumerate(

time: 40.9 us -> 39.9 us (0.976)
  Pallas kernels: 39.2 us -> 38.2 us
    pallas_call x1, Pallas kernels: 39.2 us -> 38.2 us  [local(): pl.pallas_call(kernel, out_shape=jax.ShapeDtypeStruct((128, 512), BF16),...]
where the time goes in v2:
time: 39.9 us; the launch traced here: 39.8 us
  Pallas kernels  38.2 us (96%)
  local copies, waits for them, and re-layouts  1.57 us (4%)
    pallas_call x1, Pallas kernels, local(): pl.pallas_call(kernel, out_shape=jax.ShapeDtypeStruct((128, 512), BF16),...  38.2 us
    unnamed x1, local copies, waits for them, and re-layouts  1.57 us

profile of v2, /device:TPU:1, one launch (start us, length us, event | category | flops | bytes accessed | tf_op | source)
XLA Modules:
  0.0 39.8 jit_solution(91890779714814718)
XLA Ops:
  0.0 38.2 %hyena.1 = bf16[128,512]{1,0:T(8,128)(2,1)} custom-call(bf16[3,128,512]{2,1,0:T(8,128)(2,1)} %feat.1, f32[128,512]{1,0:T(8,128)} %taps.1, f32[3,3,128]{2,1,0:T(4,128)} %bitcast.2, f32[1,128]{1,0:T(1,128)} %bitcast.3, bf16[128,1024]{1,0:T(8,128)(2,1)} %w.1, bf16[256,256]{1,0:T(8,128)(2,1)} %constant.10.clone.e1h, bf16[2,256,256]{2,1,0:T(8,128)(2,1)} %constant.11.clone.m2h, ...), custom_call_target="tpu_custom_call" | custom-call | tf_op jit(solution)/shard_map/hyena/pallas_call | solution.py:328
  38.2 1.6 %copy.12 = bf16[128,512]{1,0:T(8,128)(2,1)} copy(bf16[128,512]{1,0:T(8,128)(2,1)} %hyena.1) | data formatting | bytes 262144

commit v3 on v2

--- a/solution.py
+++ b/solution.py
@@ -10,7 +10,7 @@
 
 NP = 32
 NC = 4
-FAR_H, FAR_G, FAR_C = False, True, False
+RELAYED, LAG = 6, 8
 MESH = pl.DeviceIdType.MESH
 F32 = jnp.float32
 BF16 = jnp.bfloat16
@@ -137,9 +137,6 @@
              (m3h, m3), (bkh, bk)]
         )
     ]
-    for c in local:
-        c.start()
-
     barrier = pltpu.get_barrier_semaphore()
 
     def greet(peer):
@@ -151,6 +148,8 @@
     visit(greet, True)
     for other in (partner, up, down, across):
         pl.semaphore_signal(barrier, inc=1, device_id={"ch": other}, device_id_type=MESH)
+    for c in local:
+        c.start()
 
     local[0].wait()
     for a in range(4):
@@ -186,7 +185,7 @@
         )
 
     most = pl.ds(0, NP - 1)
-    spread(hsend, hrecv, 0, FAR_H)
+    spread(hsend, hrecv, 0, False)
     local[4].wait()
     swap = [mates(0, wv, wr)]
     swap[0].start()
@@ -225,7 +224,7 @@
     rows[pl.ds(0, 128, stride=4), :] = gt[0, :, :128]
     gsend[...] = rows[...].astype(BF16).reshape(NP, 16, 128)
     grecv[me] = gsend[me]
-    spread(gsend, grecv, 1, FAR_G)
+    spread(gsend, grecv, 1, True)
     for half in range(2):
         gt[half] = col[:, 9:10] * gt[half]
     whole = short(0, edge(0), 512)
@@ -260,7 +259,7 @@
         for half in range(2):
             half_of(peer, half, osem.at[2])
 
-    visit(both_of, FAR_C)
+    visit(both_of, False)
 
     planes = [lax.rem(z + d, 8) for d in (0, 1, 7, 2, 6, 3, 5, 4)]
 
@@ -271,7 +270,13 @@
         )
 
     sent = []
-    for k in (range(7, -1, -1) if FAR_C else range(8)):
+
+    def go(*args):
+        copy = hand(*args)
+        copy.start()
+        sent.append(copy)
+
+    def own(k):
         first = planes[k]
         arrived(crecv.at[0, pl.ds(0, 8 if k else 7)], csem.at[first])
         here = pl.ds(pl.multiple_of(16 * first, 16), 16)
@@ -287,26 +292,44 @@
                 ag[2 * y + block, here, lanes] = (
                     f[here, lanes] * (conv + g[here, lanes])
                 ).astype(BF16)
-        for t, other in ((2, across), (0, up), (1, down)):
-            copy = hand(y, k, t, other)
-            copy.start()
-            sent.append(copy)
+        if k >= RELAYED:
+            go(y, k, 2, across)
+        go(y, k, k % 2, (up, down)[k % 2])
+        go(y, k, 1 - k % 2, (down, up)[k % 2])
+
+    taken = set()
+
+    def take(t, k):
+        if (t, k) not in taken:
+            taken.add((t, k))
+            other = (down, up, across)[t]
+            hand(lax.div(other, 2), k, t, other).wait_recv()
+
+    def relay(k):
+        take(k % 2, k)
+        go(lax.div((down, up)[k % 2], 2), k, 2, (up, down)[k % 2])
+
+    for step in range(8 + LAG):
+        if step < 8:
+            own(step)
+        if 0 <= step - LAG < RELAYED:
+            relay(step - LAG)
 
     def pair(chip):
         both = ag[pl.ds(2 * chip, 2)].reshape(256, 256)
         columns = pl.ds(pl.multiple_of(256 * chip, 256), 256)
-        return dot(jnp.concatenate([wr[:, columns], wv[:, columns]], 0), both)
-
-    total = pair(y)
+        return dot(wr[:, columns], both), dot(wv[:, columns], both)
+
+    theirs, mine = pair(y)
     for t, other in ((0, down), (1, up), (2, across)):
         for k in range(8):
-            hand(other // 2, k, t, other).wait_recv()
-        total = total + pair(other // 2)
-    fin[...] = total[:128].astype(BF16)
+            take(t, k)
+        more = pair(lax.div(other, 2))
+        theirs, mine = theirs + more[0], mine + more[1]
+    fin[...] = theirs.astype(BF16)
     last = mates(3, fin, finr)
     last.start()
-    mine = total[128:].astype(BF16)
-    out[:, pl.ds(pl.multiple_of(256 * core, 256), 256)] = mine
+    out[:, pl.ds(pl.multiple_of(256 * core, 256), 256)] = mine.astype(BF16)
     last.wait_recv()
     out[:, pl.ds(pl.multiple_of(256 * (1 - core), 256), 256)] = finr[...]
 

time: 39.9 us -> 39.3 us (0.985)
  Pallas kernels: 38.2 us -> 37.6 us
    pallas_call x1, Pallas kernels: 38.2 us -> 37.6 us  [local(): pl.pallas_call(kernel, out_shape=jax.ShapeDtypeStruct((128, 512), BF16),...]
where the time goes in v3:
time: 39.3 us; the launch traced here: 39.2 us
  Pallas kernels  37.6 us (96%)
  local copies, waits for them, and re-layouts  1.57 us (4%)
    pallas_call x1, Pallas kernels, local(): pl.pallas_call(kernel, out_shape=jax.ShapeDtypeStruct((128, 512), BF16),...  37.6 us
    unnamed x1, local copies, waits for them, and re-layouts  1.57 us

profile of v3, /device:TPU:1, one launch (start us, length us, event | category | flops | bytes accessed | tf_op | source)
XLA Modules:
  0.0 39.2 jit_solution(18157288535521993913)
XLA Ops:
  0.0 37.6 %hyena.1 = bf16[128,512]{1,0:T(8,128)(2,1)} custom-call(bf16[3,128,512]{2,1,0:T(8,128)(2,1)} %feat.1, f32[128,512]{1,0:T(8,128)} %taps.1, f32[3,3,128]{2,1,0:T(4,128)} %bitcast.2, f32[1,128]{1,0:T(1,128)} %bitcast.3, bf16[128,1024]{1,0:T(8,128)(2,1)} %w.1, bf16[256,256]{1,0:T(8,128)(2,1)} %constant.10.clone.e1h, bf16[2,256,256]{2,1,0:T(8,128)(2,1)} %constant.11.clone.m2h, ...), custom_call_target="tpu_custom_call" | custom-call | tf_op jit(solution)/shard_map/hyena/pallas_call | solution.py:351
  37.6 1.6 %copy.12 = bf16[128,512]{1,0:T(8,128)(2,1)} copy(bf16[128,512]{1,0:T(8,128)(2,1)} %hyena.1) | data formatting | bytes 262144

commit v4 on v3

--- a/solution.py
+++ b/solution.py
@@ -10,7 +10,7 @@
 
 NP = 32
 NC = 4
-RELAYED, LAG = 6, 8
+RELAYED, LAG = 6, 6
 MESH = pl.DeviceIdType.MESH
 F32 = jnp.float32
 BF16 = jnp.bfloat16
@@ -81,7 +81,7 @@
     done = dot(back[0], high) + dot(back[1], high) + dot(back[0], low)
     for c in range(NC):
         for a in range(4):
-            rows[pl.ds(a // 2 * 8 + 2 * c + a % 2, NP, stride=16), :] = done[
+            rows[pl.ds(4 * c + a, NP, stride=16), :] = done[
                 NP * a : NP * a + NP, 128 * c : 128 * c + 128
             ]
 
@@ -98,7 +98,7 @@
 def kernel(
     feat, taps, sw, skip, w, e1h, m2h, m3h, bkh, twh, out,
     fv, tv, swv, skv, wv, wr, e1, m2, m3, bk, tw,
-    rimsend, rimrecv, cols, f0, gt, f0r, gtr, rows,
+    rimsend, rimrecv, cols, f0, gt, rows,
     hsend, hrecv, gsend, grecv, csend, crecv, spec, ag, fin, finr,
     lsem, osem, rsem, csem, asem, arem, psem, prem,
 ):
@@ -140,10 +140,7 @@
     barrier = pltpu.get_barrier_semaphore()
 
     def greet(peer):
-        for own in (ch, partner):
-            pl.semaphore_signal(
-                barrier, inc=1, device_id={"ctx": peer, "ch": own}, device_id_type=MESH
-            )
+        pl.semaphore_signal(barrier, inc=1, device_id={"ctx": peer}, device_id_type=MESH)
 
     visit(greet, True)
     for other in (partner, up, down, across):
@@ -160,17 +157,17 @@
     for s in range(3):
         rimsend[pl.ds(8 * s, 8), :] = fv[s, :, 384:].astype(F32).T[120:, :]
 
-    pl.semaphore_wait(barrier, 2 * (NP - 1) + 4)
+    pl.semaphore_wait(barrier, NP - 1 + 4)
     rim = pltpu.make_async_remote_copy(
         rimsend, rimrecv, osem.at[3], rsem.at[3],
         device_id={"ctx": lax.rem(me + 1, NP)}, device_id_type=MESH,
     )
     rim.start()
 
-    def spread(send, recv, k, far):
+    def spread(send, recv, k, sem, far):
         def one(peer):
             pltpu.make_async_remote_copy(
-                send.at[peer], recv.at[me], osem.at[k], rsem.at[k],
+                send.at[peer], recv.at[me], osem.at[k], sem,
                 device_id={"ctx": peer}, device_id_type=MESH,
             ).start()
 
@@ -185,10 +182,10 @@
         )
 
     most = pl.ds(0, NP - 1)
-    spread(hsend, hrecv, 0, False)
+    spread(hsend, hrecv, 0, rsem.at[0], False)
     local[4].wait()
-    swap = [mates(0, wv, wr)]
-    swap[0].start()
+    swap = mates(0, wv, wr)
+    swap.start()
 
     local[2].wait()
     local[3].wait()
@@ -208,10 +205,9 @@
         return total
 
     nothing = jnp.zeros((128, 128), F32)
-    gated = short(1, nothing, 512) * short(2, nothing, 512)
-    gt[0], gt[1] = gated[:, :256], gated[:, 256:]
+    gt[...] = short(1, nothing, 512) * short(2, nothing, 512)
     for a in range(1, 4):
-        rows[pl.ds(a, 128, stride=4), :] = gated[:, 128 * a : 128 * a + 128]
+        rows[pl.ds(a, 128, stride=4), :] = gt[:, 128 * a : 128 * a + 128]
 
     rim.wait()
     inside = me > 0
@@ -220,51 +216,32 @@
         last = jnp.concatenate([jnp.zeros((120, 128), F32), rimrecv[pl.ds(8 * s, 8), :]], 0)
         return jnp.where(inside, last.T, 0.0)
 
-    gt[0, :, :128] = short(1, edge(1), 128) * short(2, edge(2), 128)
-    rows[pl.ds(0, 128, stride=4), :] = gt[0, :, :128]
+    gt[:, :128] = short(1, edge(1), 128) * short(2, edge(2), 128)
+    rows[pl.ds(0, 128, stride=4), :] = gt[:, :128]
     gsend[...] = rows[...].astype(BF16).reshape(NP, 16, 128)
     grecv[me] = gsend[me]
-    spread(gsend, grecv, 1, True)
-    for half in range(2):
-        gt[half] = col[:, 9:10] * gt[half]
-    whole = short(0, edge(0), 512)
-    f0[0], f0[1] = whole[:, :256], whole[:, 256:]
-    swap += [mates(1, gt.at[1 - core], gtr), mates(2, f0.at[1 - core], f0r)]
-    swap[1].start()
-    swap[2].start()
+    spread(gsend, grecv, 1, rsem.at[1], True)
+    gt[...] = col[:, 9:10] * gt[...]
+    f0[...] = short(0, edge(0), 512)
 
     for c in local[5:]:
         c.wait()
     arrived(hrecv.at[most], rsem.at[0])
     rows[...] = hrecv[...].reshape(512, 128).astype(F32)
     spec[...] = forward(rows, e1, m2, tw)
-    for c in swap:
-        c.wait_recv()
+    swap.wait_recv()
     arrived(grecv.at[most], rsem.at[1])
     rows[...] = grecv[...].reshape(512, 128).astype(F32)
     inverse(product(forward(rows, e1, m2, tw), spec[...]), rows, m3, bk, tw)
 
-    csend[...] = rows[...].astype(BF16).reshape(NP, 2, 8, 128)
-    crecv[core, me] = csend[me, core]
-
-    def half_of(peer, half, sem):
-        pltpu.make_async_remote_copy(
-            csend.at[peer, half], crecv.at[core, me], sem, csem.at[z],
-            device_id={"ctx": peer, "ch": 2 * y + half}, device_id_type=MESH,
-        ).start()
-
-    half_of(me, 1 - core, osem.at[4])
-
-    def both_of(peer):
-        for half in range(2):
-            half_of(peer, half, osem.at[2])
-
-    visit(both_of, False)
+    csend[...] = rows[...].astype(BF16).reshape(NP, 16, 128)
+    crecv[me] = csend[me]
+    spread(csend, crecv, 2, csem.at[z], False)
 
     planes = [lax.rem(z + d, 8) for d in (0, 1, 7, 2, 6, 3, 5, 4)]
 
     def hand(chip, k, t, other):
-        piece = ag.at[pl.ds(2 * chip, 2), pl.ds(pl.multiple_of(16 * planes[k], 16), 16)]
+        piece = ag.at[chip, pl.ds(pl.multiple_of(16 * planes[k], 16), 16)]
         return pltpu.make_async_remote_copy(
             piece, piece, asem.at[t, k], arem.at[t, k], device_id={"ch": other}, device_id_type=MESH
         )
@@ -278,20 +255,14 @@
 
     def own(k):
         first = planes[k]
-        arrived(crecv.at[0, pl.ds(0, 8 if k else 7)], csem.at[first])
+        arrived(crecv.at[pl.ds(0, 4 if k else 3)], csem.at[first])
         here = pl.ds(pl.multiple_of(16 * first, 16), 16)
-        for which, (block, f, g) in enumerate(
-            [(core, f0.at[core], gt.at[core]), (1 - core, f0r, gtr)]
-        ):
-            base = 64 * k + 32 * which
-            came = crecv[block, pl.ds(4 * first, 4)].reshape(32, 128)
-            rows[pl.ds(base, 32), :] = came.astype(F32)
-            for a in range(2):
-                lanes = pl.ds(128 * a, 128)
-                conv = rows[pl.ds(base + a, 16, stride=2), :]
-                ag[2 * y + block, here, lanes] = (
-                    f[here, lanes] * (conv + g[here, lanes])
-                ).astype(BF16)
+        came = crecv[pl.ds(4 * first, 4)].reshape(64, 128)
+        rows[pl.ds(64 * k, 64), :] = came.astype(F32)
+        for a in range(4):
+            lanes = pl.ds(128 * a, 128)
+            conv = rows[pl.ds(64 * k + a, 16, stride=4), :]
+            ag[y, here, lanes] = (f0[here, lanes] * (conv + gt[here, lanes])).astype(BF16)
         if k >= RELAYED:
             go(y, k, 2, across)
         go(y, k, k % 2, (up, down)[k % 2])
@@ -315,30 +286,27 @@
         if 0 <= step - LAG < RELAYED:
             relay(step - LAG)
 
-    def pair(chip):
-        both = ag[pl.ds(2 * chip, 2)].reshape(256, 256)
-        columns = pl.ds(pl.multiple_of(256 * chip, 256), 256)
-        return dot(wr[:, columns], both), dot(wv[:, columns], both)
-
-    theirs, mine = pair(y)
+    def term(chip):
+        columns = pl.ds(pl.multiple_of(256 * chip + 128 * core, 128), 128)
+        return dot(wr[:, columns], ag[chip]), dot(wv[:, columns], ag[chip])
+
+    theirs, mine = term(y)
     for t, other in ((0, down), (1, up), (2, across)):
         for k in range(8):
             take(t, k)
-        more = pair(lax.div(other, 2))
+        more = term(lax.div(other, 2))
         theirs, mine = theirs + more[0], mine + more[1]
-    fin[...] = theirs.astype(BF16)
-    last = mates(3, fin, finr)
+    fin[...] = theirs
+    last = mates(1, fin, finr)
     last.start()
-    out[:, pl.ds(pl.multiple_of(256 * core, 256), 256)] = mine.astype(BF16)
     last.wait_recv()
-    out[:, pl.ds(pl.multiple_of(256 * (1 - core), 256), 256)] = finr[...]
-
-    for copy in sent + swap + [last]:
+    out[...] = (mine + finr[...]).astype(BF16)
+
+    for copy in sent + [swap, last]:
         copy.wait_send()
     arrived(hsend.at[most], osem.at[0])
     arrived(gsend.at[most], osem.at[1])
     arrived(csend.at[most], osem.at[2])
-    arrived(csend.at[0, 0], osem.at[4])
 
 
 def local(featurized, short_weights, filter_taps, skip_gain, w_out):
@@ -346,8 +314,7 @@
     far = pl.BlockSpec(memory_space=pl.ANY)
     V = pltpu.VMEM
     chunk = V((NP, 16, 128), BF16)
-    two = V((2, 128, 256), F32)
-    half = V((128, 256), F32)
+    block = V((128, 512), F32)
     return pl.pallas_call(
         kernel,
         out_shape=jax.ShapeDtypeStruct((128, 512), BF16),
@@ -359,17 +326,17 @@
             V(e1.shape, BF16), V(m2.shape, BF16), V(m3.shape, BF16),
             V(back.shape, BF16), V(twist.shape, F32),
             V((24, 128), F32), V((24, 128), F32), V((128, 128), F32),
-            two, two, half, half, V((512, 128), F32), chunk, chunk, chunk, chunk,
-            V((NP, 2, 8, 128), BF16), V((2, NP, 8, 128), BF16),
-            V((512, 256), F32), V((8, 128, 256), BF16), V((128, 256), BF16), V((128, 256), BF16),
+            block, block, V((512, 128), F32), chunk, chunk, chunk, chunk,
+            chunk, chunk,
+            V((512, 256), F32), V((4, 128, 512), BF16), block, block,
             pltpu.SemaphoreType.DMA((10,)),
-            pltpu.SemaphoreType.DMA((5,)),
+            pltpu.SemaphoreType.DMA((4,)),
             pltpu.SemaphoreType.DMA((4,)),
             pltpu.SemaphoreType.DMA((8,)),
             pltpu.SemaphoreType.DMA((3, 8)),
             pltpu.SemaphoreType.DMA((3, 8)),
-            pltpu.SemaphoreType.DMA((4,)),
-            pltpu.SemaphoreType.DMA((4,)),
+            pltpu.SemaphoreType.DMA((2,)),
+            pltpu.SemaphoreType.DMA((2,)),
         ],
         compiler_params=pltpu.CompilerParams(collective_id=0, has_side_effects=True),
         name="hyena",

time: 39.3 us -> 38.7 us (0.985)
  Pallas kernels: 37.6 us -> 37 us
    pallas_call x1, Pallas kernels: 37.6 us -> 37 us  [local(): pl.pallas_call(kernel, out_shape=jax.ShapeDtypeStruct((128, 512), BF16),...]
where the time goes in v4:
time: 38.7 us; the launch traced here: 38.6 us
  Pallas kernels  37 us (96%)
  local copies, waits for them, and re-layouts  1.57 us (4%)
    pallas_call x1, Pallas kernels, local(): pl.pallas_call(kernel, out_shape=jax.ShapeDtypeStruct((128, 512), BF16),...  37 us
    unnamed x1, local copies, waits for them, and re-layouts  1.57 us

profile of v4, /device:TPU:1, one launch (start us, length us, event | category | flops | bytes accessed | tf_op | source)
XLA Modules:
  0.0 38.6 jit_solution(4916439515649922404)
XLA Ops:
  0.0 37.0 %hyena.1 = bf16[128,512]{1,0:T(8,128)(2,1)} custom-call(bf16[3,128,512]{2,1,0:T(8,128)(2,1)} %feat.1, f32[128,512]{1,0:T(8,128)} %taps.1, f32[3,3,128]{2,1,0:T(4,128)} %bitcast.2, f32[1,128]{1,0:T(1,128)} %bitcast.3, bf16[128,1024]{1,0:T(8,128)(2,1)} %w.1, bf16[256,256]{1,0:T(8,128)(2,1)} %constant.10.clone.e1h, bf16[2,256,256]{2,1,0:T(8,128)(2,1)} %constant.11.clone.m2h, ...), custom_call_target="tpu_custom_call" | custom-call | tf_op jit(solution)/shard_map/hyena/pallas_call | solution.py:318
  37.0 1.6 %copy.12 = bf16[128,512]{1,0:T(8,128)(2,1)} copy(bf16[128,512]{1,0:T(8,128)(2,1)} %hyena.1) | data formatting | bytes 262144

commit v5 on v4

--- a/solution.py
+++ b/solution.py
@@ -66,19 +66,19 @@
         re, im = mixed[:128, 128 * c : 128 * c + 128], mixed[128:, 128 * c : 128 * c + 128]
         turned.append(jnp.concatenate([re * tr - im * ti, re * ti + im * tr], 1))
     high, low = halves(jnp.concatenate(turned, 0))
-    return dot(high, m2[0]) + dot(low, m2[0]) + dot(high, m2[1])
+    return dot(jnp.concatenate([high, low, high], 1), jnp.concatenate([m2[0], m2[0], m2[1]], 0))
 
 
 def inverse(spectrum, rows, m3, back, twist):
     high, low = halves(spectrum)
-    mixed = dot(high, m3[0]) + dot(low, m3[0]) + dot(high, m3[1])
+    mixed = dot(jnp.concatenate([high, low, high], 1), jnp.concatenate([m3[0], m3[0], m3[1]], 0))
     tr, ti = twist[0], twist[1]
     turned = []
     for c in range(NC):
         re, im = mixed[128 * c : 128 * c + 128, :128], mixed[128 * c : 128 * c + 128, 128:]
         turned.append(jnp.concatenate([re * tr + im * ti, im * tr - re * ti], 0))
     high, low = halves(jnp.concatenate(turned, 1))
-    done = dot(back[0], high) + dot(back[1], high) + dot(back[0], low)
+    done = dot(jnp.concatenate([back[0], back[1], back[0]], 1), jnp.concatenate([high, high, low], 0))
     for c in range(NC):
         for a in range(4):
             rows[pl.ds(4 * c + a, NP, stride=16), :] = done[
@@ -338,7 +338,7 @@
             pltpu.SemaphoreType.DMA((2,)),
             pltpu.SemaphoreType.DMA((2,)),
         ],
-        compiler_params=pltpu.CompilerParams(collective_id=0, has_side_effects=True),
+        compiler_params=pltpu.CompilerParams(collective_id=0, has_side_effects=True, vmem_limit_bytes=56350000),
         name="hyena",
     )(
         featurized, filter_taps, jnp.swapaxes(short_weights, 1, 2), skip_gain.reshape(1, 128),

time: 38.7 us -> 38.4 us (level)
  Pallas kernels: 37 us -> 36.3 us
  local copies, waits for them, and re-layouts: 1.57 us -> 2 us
    pallas_call x1, Pallas kernels: 37 us -> 36.3 us  [local(): pl.pallas_call(kernel, out_shape=jax.ShapeDtypeStruct((128, 512), BF16),...]
    unnamed x1 -> x5, local copies, waits for them, and re-layouts: 1.57 us -> 2 us
where the time goes in v5:
time: 38.4 us; the launch traced here: 38.3 us
  Pallas kernels  36.3 us (95%)
  local copies, waits for them, and re-layouts  2 us (5%)
    pallas_call x1, Pallas kernels, local(): pl.pallas_call(kernel, out_shape=jax.ShapeDtypeStruct((128, 512), BF16),...  36.3 us
    unnamed x5, local copies, waits for them, and re-layouts  2 us

profile of v5, /device:TPU:1, one launch (start us, length us, event | category | flops | bytes accessed | tf_op | source)
XLA Modules:
  0.0 38.3 jit_solution(10122193046123694832)
XLA Ops:
  0.0 0.0 copy-start.1
  0.0 0.7 %copy-done.1 = f32[128]{0:T(128)S(1)} copy-done((f32[128]{0:T(128)S(1)}, f32[128]{0:T(128)}, u32[]{:S(2)}) %copy-start.1) | copy-done | bytes 536
  0.7 0.0 copy-start
  0.7 0.7 %copy-done = f32[3,128,3]{1,2,0:T(4,128)S(1)} copy-done((f32[3,128,3]{1,2,0:T(4,128)S(1)}, f32[3,128,3]{1,2,0:T(4,128)}, u32[]{:S(2)}) %copy-start) | copy-done | bytes 4632
  1.3 36.3 %hyena.1 = bf16[128,512]{1,0:T(8,128)(2,1)S(1)} custom-call(bf16[3,128,512]{2,1,0:T(8,128)(2,1)} %feat.1, f32[128,512]{1,0:T(8,128)} %taps.1, f32[3,3,128]{2,1,0:T(4,128)S(1)} %bitcast.2, f32[1,128]{1,0:T(1,128)S(1)} %bitcast.3, bf16[128,1024]{1,0:T(8,128)(2,1)} %w.1, bf16[256,256]{1,0:T(8,128)(2,1)} %constant.10.clone.e1h, ...), custom_call_target="tpu_custom_call" | custom-call | tf_op jit(solution)/shard_map/hyena/pallas_call | solution.py:318
  37.6 0.7 %copy.12 = bf16[128,512]{1,0:T(8,128)(2,1)} copy(bf16[128,512]{1,0:T(8,128)(2,1)S(1)} %hyena.1) | data formatting | bytes 262144
Async XLA Ops:
  0.0 0.7 %copy-start.1 = (f32[128]{0:T(128)S(1)}, f32[128]{0:T(128)}, u32[]{:S(2)}) copy-start(f32[128]{0:T(128)} %param.13) | copy-start | bytes 1540
  0.7 0.7 %copy-start = (f32[3,128,3]{1,2,0:T(4,128)S(1)}, f32[3,128,3]{1,2,0:T(4,128)}, u32[]{:S(2)}) copy-start(f32[3,128,3]{1,2,0:T(4,128)} %param.11) | copy-start | bytes 13828

commit v6 on v5

--- a/solution.py
+++ b/solution.py
@@ -157,36 +157,6 @@
     for s in range(3):
         rimsend[pl.ds(8 * s, 8), :] = fv[s, :, 384:].astype(F32).T[120:, :]
 
-    pl.semaphore_wait(barrier, NP - 1 + 4)
-    rim = pltpu.make_async_remote_copy(
-        rimsend, rimrecv, osem.at[3], rsem.at[3],
-        device_id={"ctx": lax.rem(me + 1, NP)}, device_id_type=MESH,
-    )
-    rim.start()
-
-    def spread(send, recv, k, sem, far):
-        def one(peer):
-            pltpu.make_async_remote_copy(
-                send.at[peer], recv.at[me], osem.at[k], sem,
-                device_id={"ctx": peer}, device_id_type=MESH,
-            ).start()
-
-        visit(one, far)
-
-    def arrived(part, sem):
-        pltpu.make_async_copy(part, part, sem).wait()
-
-    def mates(i, source, target):
-        return pltpu.make_async_remote_copy(
-            source, target, psem.at[i], prem.at[i], device_id={"ch": partner}, device_id_type=MESH
-        )
-
-    most = pl.ds(0, NP - 1)
-    spread(hsend, hrecv, 0, rsem.at[0], False)
-    local[4].wait()
-    swap = mates(0, wv, wr)
-    swap.start()
-
     local[2].wait()
     local[3].wait()
     cols[...] = jnp.zeros_like(cols)
@@ -208,6 +178,36 @@
     gt[...] = short(1, nothing, 512) * short(2, nothing, 512)
     for a in range(1, 4):
         rows[pl.ds(a, 128, stride=4), :] = gt[:, 128 * a : 128 * a + 128]
+
+    pl.semaphore_wait(barrier, NP - 1 + 4)
+    rim = pltpu.make_async_remote_copy(
+        rimsend, rimrecv, osem.at[3], rsem.at[3],
+        device_id={"ctx": lax.rem(me + 1, NP)}, device_id_type=MESH,
+    )
+    rim.start()
+
+    def spread(send, recv, k, sem, far):
+        def one(peer):
+            pltpu.make_async_remote_copy(
+                send.at[peer], recv.at[me], osem.at[k], sem,
+                device_id={"ctx": peer}, device_id_type=MESH,
+            ).start()
+
+        visit(one, far)
+
+    def arrived(part, sem):
+        pltpu.make_async_copy(part, part, sem).wait()
+
+    def mates(i, source, target):
+        return pltpu.make_async_remote_copy(
+            source, target, psem.at[i], prem.at[i], device_id={"ch": partner}, device_id_type=MESH
+        )
+
+    most = pl.ds(0, NP - 1)
+    spread(hsend, hrecv, 0, rsem.at[0], False)
+    local[4].wait()
+    swap = mates(0, wv, wr)
+    swap.start()
 
     rim.wait()
     inside = me > 0

time: 38.4 us -> 38.4 us (level)
  no operation moved by 1% of the time
where the time goes in v6:
time: 38.4 us; the launch traced here: 38.3 us
  Pallas kernels  36.3 us (95%)
  local copies, waits for them, and re-layouts  2 us (5%)
    pallas_call x1, Pallas kernels, local(): pl.pallas_call(kernel, out_shape=jax.ShapeDtypeStruct((128, 512), BF16),...  36.3 us
    unnamed x5, local copies, waits for them, and re-layouts  2 us

profile of v6, /device:TPU:1, one launch (start us, length us, event | category | flops | bytes accessed | tf_op | source)
XLA Modules:
  0.0 38.3 jit_solution(13210424427693333488)
XLA Ops:
  0.0 0.0 copy-start.1
  0.0 0.7 %copy-done.1 = f32[128]{0:T(128)S(1)} copy-done((f32[128]{0:T(128)S(1)}, f32[128]{0:T(128)}, u32[]{:S(2)}) %copy-start.1) | copy-done | bytes 536
  0.7 0.0 copy-start
  0.7 0.7 %copy-done = f32[3,128,3]{1,2,0:T(4,128)S(1)} copy-done((f32[3,128,3]{1,2,0:T(4,128)S(1)}, f32[3,128,3]{1,2,0:T(4,128)}, u32[]{:S(2)}) %copy-start) | copy-done | bytes 4632
  1.3 36.3 %hyena.1 = bf16[128,512]{1,0:T(8,128)(2,1)S(1)} custom-call(bf16[3,128,512]{2,1,0:T(8,128)(2,1)} %feat.1, f32[128,512]{1,0:T(8,128)} %taps.1, f32[3,3,128]{2,1,0:T(4,128)S(1)} %bitcast.2, f32[1,128]{1,0:T(1,128)S(1)} %bitcast.3, bf16[128,1024]{1,0:T(8,128)(2,1)} %w.1, bf16[256,256]{1,0:T(8,128)(2,1)} %constant.10.clone.e1h, ...), custom_call_target="tpu_custom_call" | custom-call | tf_op jit(solution)/shard_map/hyena/pallas_call | solution.py:318
  37.7 0.7 %copy.12 = bf16[128,512]{1,0:T(8,128)(2,1)} copy(bf16[128,512]{1,0:T(8,128)(2,1)S(1)} %hyena.1) | data formatting | bytes 262144
Async XLA Ops:
  0.0 0.7 %copy-start.1 = (f32[128]{0:T(128)S(1)}, f32[128]{0:T(128)}, u32[]{:S(2)}) copy-start(f32[128]{0:T(128)} %param.13) | copy-start | bytes 1540
  0.7 0.7 %copy-start = (f32[3,128,3]{1,2,0:T(4,128)S(1)}, f32[3,128,3]{1,2,0:T(4,128)}, u32[]{:S(2)}) copy-start(f32[3,128,3]{1,2,0:T(4,128)} %param.11) | copy-start | bytes 13828
